TPU v7x, 32 devices: a whole 2x2x4 slice. The times are simulated.
32 devices in a mesh: dp: 8 (over z, y), mp: 4 (over x, core).
Axes of the slice: x: 2, y: 2, z: 4, core: 2. Of those that a mesh axis runs over, the one named last changes fastest.
Arguments:
- pred_input: bfloat16 [512, 256, 384], P('dp'), may hold values from -6 to 6
- proj_weight: bfloat16 [384, 1280], P('dp', 'mp'), may hold values from -0.3125 to 0.3125
- proj_bias: float32 [1280], P('mp'), may hold values from -3 to 3
- targets: bfloat16 [512, 256, 1280], P('dp', None, 'mp'), may hold values from -6 to 6
- block_masks: int32 [512, 4, 256], P('dp'), may hold values from 0 to 1, as said below
Outputs:
- loss: float32 [], replicated
- clip_scale: float32 [], replicated
- grad_weight: float32 [384, 1280], P('dp', 'mp')
- grad_bias: float32 [1280], P('mp')
Inputs may be any that keep to these rules, and one draw needn't show every extreme that they name: `block_masks`: each of an image's 4 target blocks is a nonempty rectangle of patches on the 16 x 16 grid (row-major patch order); blocks may intersect.
All inputs are finite; a program needn't handle non-finite values.
Results may differ from a plain program's by a relative error of at most 0.0003.
Values may be sent and summed in bfloat16 or wider, within the bound.
A program may use at most 192 MiB of HBM per device.

v0:
```python
import jax
import jax.numpy as jnp
from jax import lax
from jax.sharding import PartitionSpec as P


def body(pred_input, proj_weight, proj_bias, targets, block_masks):
    images_here, patches, pred_width = pred_input.shape
    feat_local = targets.shape[2]
    feat_full = feat_local * lax.axis_size("mp")
    token_count = images_here * patches
    coverage = jnp.sum(block_masks, axis=1).astype(jnp.float32)
    share = patches // lax.axis_size("mp")
    owned_cover = lax.dynamic_slice_in_dim(coverage, lax.axis_index("mp") * share, share, 1)
    count_part = jnp.sum(owned_cover)
    target_f = targets.astype(jnp.float32).reshape(token_count, feat_local)
    feat_sums, feat_squares = lax.psum(
        (jnp.sum(target_f, axis=1), jnp.sum(target_f * target_f, axis=1)), "mp"
    )
    mean_feat = feat_sums / feat_full
    variance = feat_squares / feat_full - mean_feat * mean_feat
    tnorm = (target_f - mean_feat[:, None]) * lax.rsqrt(variance[:, None] + 1e-05)
    inputs_flat = pred_input.reshape(token_count, pred_width)
    weight_full = lax.all_gather(proj_weight, "dp", axis=0, tiled=True)
    pred = jnp.dot(inputs_flat, weight_full, preferred_element_type=jnp.float32) + proj_bias
    differ = pred - tnorm
    magnitude = jnp.abs(differ)
    smooth = jnp.where(magnitude < 1.0, 0.5 * differ * differ, magnitude - 0.5)
    cover_column = coverage.reshape(token_count, 1)
    loss_part = jnp.sum(cover_column * smooth)
    clipped = cover_column * jnp.clip(differ, -1.0, 1.0)
    source = clipped.astype(jnp.bfloat16)
    grad_full = lax.dot_general(
        inputs_flat, source, (((0,), (0,)), ((), ())), preferred_element_type=jnp.float32
    )
    bias_part = jnp.sum(clipped, axis=0)
    grad_rows = lax.psum_scatter(grad_full, "dp", scatter_dimension=0, tiled=True)
    bias_grad = lax.psum(bias_part, "dp")
    bias_square = jnp.where(lax.axis_index("dp") == 0, jnp.sum(bias_grad * bias_grad), 0.0)
    square_part = jnp.sum(grad_rows * grad_rows) + bias_square
    total = lax.psum(count_part, ("dp", "mp"))
    loss_total = lax.psum(loss_part, ("dp", "mp"))
    square_total = lax.psum(square_part, ("dp", "mp"))
    norm = jnp.sqrt(square_total) / total
    clip_scale = jnp.minimum(1.0, 1.0 / (norm + 1e-06))
    factor = clip_scale / total
    loss = loss_total / total / feat_full
    return (loss, clip_scale, grad_rows * factor, bias_grad * factor)


def solution(mesh):
    in_specs = (
        P("dp", None, None),
        P("dp", "mp"),
        P("mp"),
        P("dp", None, "mp"),
        P("dp", None, None),
    )
    out_specs = (P(), P(), P("dp", "mp"), P("mp"))
    return jax.shard_map(body, mesh=mesh, in_specs=in_specs, out_specs=out_specs, check_vma=False)
```

profile of v0, /device:TPU:0, one launch (start us, length us, event | category | flops | bytes accessed | tf_op | source)
XLA Modules:
  0.0 243.8 jit_solution(10438953832590673611)
XLA Ops:
  7.2 0.0 copy-start
  7.2 0.0 all-reduce.4.cloned.1.call-start
  7.2 9.9 %convert_reduce_fusion = (f32[64,256]{1,0:T(8,128)S(1)}, f32[64,256]{1,0:T(8,128)S(1)}) fusion(bf16[64,256,320]{1,2,0:T(8,128)(2,1)} %param.8), kind=kLoop, calls=%fused_computation.2 | loop fusion | flops 20938752 | bytes 10616832 | tf_op jit(solution)/shard_map/reduce_sum | solution.py:18
  17.2 0.7 copy.19
  17.8 0.7 copy.20
  18.5 0.0 all-reduce.4.cloned.1.call-update
  18.5 0.0 reduce-scatter.4.cloned.1.call-start
  18.5 13.9 %convert_bitcast_fusion = f32[64,40,8,256]{3,2,1,0:T(8,128)} fusion(bf16[64,256,320]{1,2,0:T(8,128)(2,1)} %param.8), kind=kLoop, calls=%fused_computation.3 | loop fusion | flops 5242880 | bytes 31457280
  32.4 0.0 copy-done
  32.4 0.2 reduce_sum.76
  32.7 0.0 copy-start.1
  32.7 0.0 copy-start.2
  32.7 15.9 %copy.17 = f32[64,40,8,256]{3,2,0,1:T(8,128)} copy(f32[64,40,8,256]{3,2,1,0:T(8,128)} %convert_bitcast_fusion) | data formatting | bytes 41943040 | tf_op jit(solution)/shard_map/reshape | solution.py:16
  48.6 0.0 copy-done.1
  48.6 32.7 %all_gather.3 = bf16[384,320]{1,0:T(8,128)(2,1)S(1)} all-gather(bf16[48,320]{1,0:T(8,128)(2,1)S(1)} %copy-done.1), channel_id=1, replica_groups=mesh['dp'=8,'mp'=4] {'dp'}, dimensions={0}, use_global_device_ids=true | all-gather | bytes 276480 | tf_op jit(solution)/shard_map/all_gather | solution.py:24
  81.3 0.0 all-reduce.4.cloned.1.call-done
  81.3 0.9 broadcast_multiply_fusion.1
  82.2 0.0 copy-done.2
  82.2 26.1 %fusion.5 = (f32[320]{0:T(512)S(1)}, f32[]{:T(128)}, f32[16384,320]{0,1:T(8,128)}) fusion(f32[16384]{0:T(1024)S(1)} %bitcast.20, f32[16384]{0:T(1024)S(1)} %get-tuple-element.28, f32[16384,320]{0,1:T(8,128)} %bitcast.19, f32[16384]{0:T(1024)S(1)} %get-tuple-element.27, f32[320]{0:T(512)S(1)} %copy-done.2, bf16[16384,384]{1,0:T(8,128)(2,1)} %bitcast.17, ...), kind=kOutput, calls=%fused_computation.11 | convolution fusion | flops 4105174784 | bytes 54970884 | tf_op jit(solution)/shard_map/dot_general | solution.py:25
  108.3 13.5 %fusion.12 = f32[384,320]{0,1:T(8,128)S(1)} fusion(bf16[16384,384]{1,0:T(8,128)(2,1)} %bitcast.18, f32[16384,320]{0,1:T(8,128)} %get-tuple-element.29, f32[16384]{0:T(1024)S(1)} %bitcast.21), kind=kOutput, calls=%fused_computation.17 | convolution fusion | flops 4042260480 | bytes 34111488 | tf_op jit(solution)/shard_map/dot_general | solution.py:33
  121.8 1.0 copy.15
  122.8 0.0 reduce-scatter.4.cloned.1.call-update
  122.9 0.7 dynamic-slice_reduce_fusion
  123.5 21.5 %psum.46 = f32[320]{0:T(512)S(1)} all-reduce(f32[320]{0:T(512)S(1)} %get-tuple-element.16), channel_id=1, replica_groups=mesh['dp'=8,'mp'=4] {'dp'}, use_global_device_ids=true, to_apply=%region_12.13 | all-reduce | flops 320 | bytes 2560 | tf_op jit(solution)/shard_map/psum | solution.py:38
  145.1 0.6 multiply_reduce_fusion.1
  146.3 40.9 %reduce-scatter.4.cloned.1.call-done = f32[48,320]{1,0:T(8,128)} async-done(((f32[384,320]{1,0:T(8,128)}), f32[48,320]{1,0:T(8,128)}) %reduce-scatter.4.cloned.1.call-update) | async-done | bytes 61456
  187.2 1.0 copy.16
  188.2 0.6 multiply_reduce_fusion
  189.5 40.3 %all-reduce = (f32[]{:T(128)}, f32[]{:T(128)}, f32[]{:T(128)}) all-reduce(f32[]{:T(128)} %get-tuple-element.17, f32[]{:T(128)} %dynamic-slice_reduce_fusion, f32[]{:T(128)S(6)} %add.44), channel_id=1, replica_groups=mesh['dp'=8,'mp'=4] {'dp','mp'}, use_global_device_ids=true, to_apply=%region_6.7 | all-reduce | flops 3 | bytes 24 | tf_op jit(solution)/shard_map/psum | solution.py:42
  232.0 0.6 broadcast_multiply_fusion.2
  233.9 0.7 copy.14
  (3 shorter events, 0.1 us)
Async XLA Ops:
  7.2 25.3 %copy-start = (s32[64,4,256]{2,1,0:T(4,128)S(1)}, s32[64,4,256]{2,1,0:T(4,128)}, u32[]{:S(2)}) copy-start(s32[64,4,256]{2,1,0:T(4,128)} %param.9) | copy-start | bytes 786436
  7.2 74.2 %all-reduce.4.cloned.1.call-start = ((), (), s32[]{:S(2)}) async-start(), calls=%async_computation.2 | async-start | bytes 262144 | tf_op jit(solution)/shard_map/psum | solution.py:17
  18.5 168.7 %reduce-scatter.4.cloned.1.call-start = ((), (), s32[]{:S(2)}) async-start(), calls=%async_computation.1 | async-start | bytes 663552
  32.7 16.0 %copy-start.1 = (bf16[48,320]{1,0:T(8,128)(2,1)S(1)}, bf16[48,320]{1,0:T(8,128)(2,1)}, u32[]{:S(2)}) copy-start(bf16[48,320]{1,0:T(8,128)(2,1)} %param.6) | copy-start | bytes 92164
  32.7 49.6 %copy-start.2 = (f32[320]{0:T(512)S(1)}, f32[320]{0:T(512)}, u32[]{:S(2)}) copy-start(f32[320]{0:T(512)} %param.7) | copy-start | bytes 3844
Sparse Core Ops, SparseCore 0:
  18.6 34.5 all-reduce.3
  123.0 64.2 reduce-scatter.3
where the time goes:
time: 244 us
  blocking collectives  94.6 us (39%)
  waiting for transfers between devices  41 us (17%)
  matrix products  39.5 us (16%)
  other arithmetic  27.4 us (11%)
  between operations  21.1 us (9%)
  local copies, waits for them, and re-layouts  20.1 us (8%)
    unnamed x3, waiting for transfers between devices  41 us
    psum x1, blocking collectives, body(): loss_total = lax.psum(loss_part, ('dp', 'mp'))  40.3 us
    all_gather x1, blocking collectives, body(): weight_full = lax.all_gather(proj_weight, 'dp', axis=0, tiled=True)  32.7 us
    dot_general x1, matrix products, body(): jnp.dot(inputs_flat, weight_full, preferred_element_type=jnp.float32)  26.1 us
    psum x1, blocking collectives, body(): bias_grad = lax.psum(bias_part, 'dp')  21.5 us
    reshape x1, local copies, waits for them, and re-layouts, body(): target_f = targets.astype(jnp.float32).reshape(token_count, feat_local)  15.9 us
    unnamed x1, other arithmetic  13.9 us
    dot_general x1, matrix products, body(): lax.dot_general(inputs_flat, source, (((0,), (0,)), ((), ())), preferred_...  13.5 us
  transfers between devices with their start and end apart: 2, of which 1 were waited for; matrix products, arithmetic and copies ran while one was open for 13% of the time, Pallas kernels for 0%

commit v1 on v0

--- a/solution.py
+++ b/solution.py
@@ -21,7 +21,12 @@
     variance = feat_squares / feat_full - mean_feat * mean_feat
     tnorm = (target_f - mean_feat[:, None]) * lax.rsqrt(variance[:, None] + 1e-05)
     inputs_flat = pred_input.reshape(token_count, pred_width)
-    weight_full = lax.all_gather(proj_weight, "dp", axis=0, tiled=True)
+    ring = [proj_weight]
+    for hop in range(7):
+        ring.append(lax.ppermute(ring[-1], "dp", [(dev, (dev + 1) % 8) for dev in range(8)]))
+    weight_full = jnp.roll(
+        jnp.concatenate(ring[::-1], axis=0), (lax.axis_index("dp") + 1) * ring[0].shape[0], axis=0
+    )
     pred = jnp.dot(inputs_flat, weight_full, preferred_element_type=jnp.float32) + proj_bias
     differ = pred - tnorm
     magnitude = jnp.abs(differ)

time: 244 us -> 238 us (0.975)
  blocking collectives: 94.6 us -> 59.8 us
  waiting for transfers between devices: 41 us -> 66.3 us
  starting transfers between devices: 0.08 us -> 4.18 us
    all_gather x1 -> x0, blocking collectives: 32.7 us -> none  [body(): weight_full = lax.all_gather(proj_weight, 'dp', axis=0, tiled=True)]
    ppermute x0 -> x7, waiting for transfers between devices: none -> 21 us  [body(): lax.ppermute(ring[-1], 'dp', [(dev, (dev + 1) % 8) for dev in range(8)])]
    ppermute x0 -> x7, starting transfers between devices: none -> 4.1 us  [body(): lax.ppermute(ring[-1], 'dp', [(dev, (dev + 1) % 8) for dev in range(8)])]
  transfers between devices with their start and end apart: 2 -> 9, of which waited for: 1 -> 6; matrix products, arithmetic and copies ran while one was open for 13% -> 18% of each run, Pallas kernels for 0% -> 0%
where the time goes in v1:
time: 238 us
  waiting for transfers between devices  66.3 us (28%)
  blocking collectives  59.8 us (25%)
  matrix products  38.7 us (16%)
  other arithmetic  27.3 us (11%)
  between operations  21.3 us (9%)
  local copies, waits for them, and re-layouts  20.2 us (8%)
  starting transfers between devices  4.18 us (2%)
    unnamed x3, waiting for transfers between devices  42.9 us
    psum x1, blocking collectives, body(): loss_total = lax.psum(loss_part, ('dp', 'mp'))  40.4 us
    dot_general x1, matrix products, body(): jnp.dot(inputs_flat, weight_full, preferred_element_type=jnp.float32)  25.3 us
    ppermute x7, waiting for transfers between devices, body(): lax.ppermute(ring[-1], 'dp', [(dev, (dev + 1) % 8) for dev in range(8)])  21 us
    psum x1, blocking collectives, body(): bias_grad = lax.psum(bias_part, 'dp')  19.4 us
    reshape x1, local copies, waits for them, and re-layouts, body(): target_f = targets.astype(jnp.float32).reshape(token_count, feat_local)  15.9 us
    unnamed x1, other arithmetic  13.9 us
    dot_general x1, matrix products, body(): lax.dot_general(inputs_flat, source, (((0,), (0,)), ((), ())), preferred_...  13.5 us
  transfers between devices with their start and end apart: 9, of which 6 were waited for; matrix products, arithmetic and copies ran while one was open for 18% of the time, Pallas kernels for 0%

profile of v1, /device:TPU:0, one launch (start us, length us, event | category | flops | bytes accessed | tf_op | source)
XLA Modules:
  0.0 237.8 jit_solution(12005120705016040503)
XLA Ops:
  7.2 0.0 copy-start
  7.2 0.0 all-reduce.4.cloned.1.call-start
  7.2 3.0 %collective-permute-start = (bf16[48,320]{1,0:T(8,128)(2,1)}, bf16[48,320]{1,0:T(8,128)(2,1)S(1)}, u32[]{:S(2)}, u32[]{:S(2)}) collective-permute-start(bf16[48,320]{1,0:T(8,128)(2,1)} %param.6), channel_id=1, source_target_pairs={{0,4},{4,8},{8,12},{12,16},{16,20},{20,24},{24,28},{28,0},{1,5},{5... | collective-permute-start | bytes 92168 | tf_op jit(solution)/shard_map/ppermute | solution.py:26
  10.3 5.2 %collective-permute-done = bf16[48,320]{1,0:T(8,128)(2,1)S(1)} collective-permute-done((bf16[48,320]{1,0:T(8,128)(2,1)}, bf16[48,320]{1,0:T(8,128)(2,1)S(1)}, u32[]{:S(2)}, u32[]{:S(2)}) %collective-permute-start) | collective-permute-done | bytes 30752 | tf_op jit(solution)/shard_map/ppermute | solution.py:26
  15.5 0.0 collective-permute-start.1
  15.5 6.7 %collective-permute-done.1 = bf16[48,320]{1,0:T(8,128)(2,1)S(1)} collective-permute-done((bf16[48,320]{1,0:T(8,128)(2,1)S(1)}, bf16[48,320]{1,0:T(8,128)(2,1)S(1)}, u32[]{:S(2)}, u32[]{:S(2)}) %collective-permute-start.1) | collective-permute-done | bytes 30752 | tf_op jit(solution)/shard_map/ppermute | solution.py:26
  22.1 0.0 collective-permute-start.2
  22.1 6.7 %collective-permute-done.2 = bf16[48,320]{1,0:T(8,128)(2,1)S(1)} collective-permute-done((bf16[48,320]{1,0:T(8,128)(2,1)S(1)}, bf16[48,320]{1,0:T(8,128)(2,1)S(1)}, u32[]{:S(2)}, u32[]{:S(2)}) %collective-permute-start.2) | collective-permute-done | bytes 30752 | tf_op jit(solution)/shard_map/ppermute | solution.py:26
  28.8 0.0 collective-permute-start.3
  28.8 9.9 %convert_reduce_fusion = (f32[64,256]{1,0:T(8,128)S(1)}, f32[64,256]{1,0:T(8,128)S(1)}) fusion(bf16[64,256,320]{1,2,0:T(8,128)(2,1)} %param.8), kind=kLoop, calls=%fused_computation.2 | loop fusion | flops 20938752 | bytes 10616832 | tf_op jit(solution)/shard_map/reduce_sum | solution.py:18
  38.7 0.7 copy.19
  39.3 0.7 copy.20
  40.0 0.0 all-reduce.4.cloned.1.call-update
  40.0 0.0 reduce-scatter.4.cloned.1.call-start
  40.1 0.0 collective-permute-done.3
  40.1 0.1 collective-permute-start.4
  40.1 13.9 %convert_bitcast_fusion = f32[64,40,8,256]{3,2,1,0:T(8,128)} fusion(bf16[64,256,320]{1,2,0:T(8,128)(2,1)} %param.8), kind=kLoop, calls=%fused_computation.3 | loop fusion | flops 5242880 | bytes 31457280
  54.0 0.0 copy-done
  54.0 0.2 reduce_sum.76
  54.2 0.0 collective-permute-done.4
  54.2 0.1 collective-permute-start.5
  54.3 0.0 copy-start.1
  54.3 0.0 copy-start.2
  54.4 15.9 %copy.17 = f32[64,40,8,256]{3,2,0,1:T(8,128)} copy(f32[64,40,8,256]{3,2,1,0:T(8,128)} %convert_bitcast_fusion) | data formatting | bytes 41943040 | tf_op jit(solution)/shard_map/reshape | solution.py:16
  70.3 0.0 collective-permute-done.5
  70.3 0.9 collective-permute-start.6
  71.2 2.4 all-reduce.4.cloned.1.call-done
  73.6 0.9 broadcast_multiply_fusion.1
  74.5 2.5 %collective-permute-done.6 = bf16[48,320]{1,0:T(8,128)(2,1)S(1)} collective-permute-done((bf16[48,320]{1,0:T(8,128)(2,1)S(1)}, bf16[48,320]{1,0:T(8,128)(2,1)S(1)}, u32[]{:S(2)}, u32[]{:S(2)}) %collective-permute-start.6) | collective-permute-done | bytes 30752 | tf_op jit(solution)/shard_map/ppermute | solution.py:26
  77.0 0.0 copy-done.1
  77.2 0.0 copy-done.2
  77.2 25.3 %fusion.6 = (f32[320]{0:T(512)S(1)}, f32[]{:T(128)}, f32[16384,320]{0,1:T(8,128)}) fusion(f32[16384]{0:T(1024)S(1)} %bitcast.23, f32[16384]{0:T(1024)S(1)} %get-tuple-element.28, f32[16384,320]{0,1:T(8,128)} %bitcast.22, f32[16384]{0:T(1024)S(1)} %get-tuple-element.27, f32[320]{0:T(512)S(1)} %copy-done.2, bf16[16384,384]{1,0:T(8,128)(2,1)} %bitcast.20, ...), kind=kOutput, calls=%fused_computation.12 | convolution fusion | flops 4105174784 | bytes 55020808 | tf_op jit(solution)/shard_map/dot_general | solution.py:30
  102.5 13.5 %fusion.13 = f32[384,320]{0,1:T(8,128)S(1)} fusion(bf16[16384,384]{1,0:T(8,128)(2,1)} %bitcast.21, f32[16384,320]{0,1:T(8,128)} %get-tuple-element.29, f32[16384]{0:T(1024)S(1)} %bitcast.24), kind=kOutput, calls=%fused_computation.18 | convolution fusion | flops 4042260480 | bytes 34111488 | tf_op jit(solution)/shard_map/dot_general | solution.py:38
  115.9 1.0 copy.15
  117.0 0.0 reduce-scatter.4.cloned.1.call-update
  117.0 0.7 dynamic-slice_reduce_fusion
  117.7 19.4 %psum.46 = f32[320]{0:T(512)S(1)} all-reduce(f32[320]{0:T(512)S(1)} %get-tuple-element.16), channel_id=1, replica_groups=mesh['dp'=8,'mp'=4] {'dp'}, use_global_device_ids=true, to_apply=%region_12.13 | all-reduce | flops 320 | bytes 2560 | tf_op jit(solution)/shard_map/psum | solution.py:43
  137.1 0.6 multiply_reduce_fusion.1
  138.4 42.9 %reduce-scatter.4.cloned.1.call-done = f32[48,320]{1,0:T(8,128)} async-done(((f32[384,320]{1,0:T(8,128)}), f32[48,320]{1,0:T(8,128)}) %reduce-scatter.4.cloned.1.call-update) | async-done | bytes 61456
  181.3 1.0 copy.16
  182.3 0.6 multiply_reduce_fusion
  183.6 40.4 %all-reduce = (f32[]{:T(128)}, f32[]{:T(128)}, f32[]{:T(128)}) all-reduce(f32[]{:T(128)} %get-tuple-element.17, f32[]{:T(128)} %dynamic-slice_reduce_fusion, f32[]{:T(128)S(6)} %add.64), channel_id=1, replica_groups=mesh['dp'=8,'mp'=4] {'dp','mp'}, use_global_device_ids=true, to_apply=%region_6.7 | all-reduce | flops 3 | bytes 24 | tf_op jit(solution)/shard_map/psum | solution.py:47
  226.0 0.6 broadcast_multiply_fusion.2
  228.0 0.7 copy.14
  (19 shorter events, 0.2 us)
Async XLA Ops:
  7.2 46.8 %copy-start = (s32[64,4,256]{2,1,0:T(4,128)S(1)}, s32[64,4,256]{2,1,0:T(4,128)}, u32[]{:S(2)}) copy-start(s32[64,4,256]{2,1,0:T(4,128)} %param.9) | copy-start | bytes 786436
  7.2 66.4 %all-reduce.4.cloned.1.call-start = ((), (), s32[]{:S(2)}) async-start(), calls=%async_computation.2 | async-start | bytes 262144 | tf_op jit(solution)/shard_map/psum | solution.py:17
  7.2 8.2 %collective-permute-start = (bf16[48,320]{1,0:T(8,128)(2,1)}, bf16[48,320]{1,0:T(8,128)(2,1)S(1)}, u32[]{:S(2)}, u32[]{:S(2)}) collective-permute-start(bf16[48,320]{1,0:T(8,128)(2,1)} %param.6), channel_id=1, source_target_pairs={{0,4},{4,8},{8,12},{12,16},{16,20},{20,24},{24,28},{28,0},{1,5},{5... | collective-permute-start | bytes 92168 | tf_op jit(solution)/shard_map/ppermute | solution.py:26
  15.5 6.7 %collective-permute-start.1 = (bf16[48,320]{1,0:T(8,128)(2,1)S(1)}, bf16[48,320]{1,0:T(8,128)(2,1)S(1)}, u32[]{:S(2)}, u32[]{:S(2)}) collective-permute-start(bf16[48,320]{1,0:T(8,128)(2,1)S(1)} %collective-permute-done), channel_id=1, source_target_pairs={{0,4},{4,8},{8,12},{12,16},{16,20},{20,24},{24,28},{28,0},{1,5},{5... | collective-permute-start | bytes 92168 | tf_op jit(solution)/shard_map/ppermute | solution.py:26
  22.1 6.7 %collective-permute-start.2 = (bf16[48,320]{1,0:T(8,128)(2,1)S(1)}, bf16[48,320]{1,0:T(8,128)(2,1)S(1)}, u32[]{:S(2)}, u32[]{:S(2)}) collective-permute-start(bf16[48,320]{1,0:T(8,128)(2,1)S(1)} %collective-permute-done.1), channel_id=1, source_target_pairs={{0,4},{4,8},{8,12},{12,16},{16,20},{20,24},{24,28},{28,0},{1,5},{5... | collective-permute-start | bytes 92168 | tf_op jit(solution)/shard_map/ppermute | solution.py:26
  28.8 11.3 %collective-permute-start.3 = (bf16[48,320]{1,0:T(8,128)(2,1)S(1)}, bf16[48,320]{1,0:T(8,128)(2,1)S(1)}, u32[]{:S(2)}, u32[]{:S(2)}) collective-permute-start(bf16[48,320]{1,0:T(8,128)(2,1)S(1)} %collective-permute-done.2), channel_id=1, source_target_pairs={{0,4},{4,8},{8,12},{12,16},{16,20},{20,24},{24,28},{28,0},{1,5},{5... | collective-permute-start | bytes 92168 | tf_op jit(solution)/shard_map/ppermute | solution.py:26
  40.0 141.3 %reduce-scatter.4.cloned.1.call-start = ((), (), s32[]{:S(2)}) async-start(), calls=%async_computation.1 | async-start | bytes 663552
  40.1 14.1 %collective-permute-start.4 = (bf16[48,320]{1,0:T(8,128)(2,1)S(1)}, bf16[48,320]{1,0:T(8,128)(2,1)S(1)}, u32[]{:S(2)}, u32[]{:S(2)}) collective-permute-start(bf16[48,320]{1,0:T(8,128)(2,1)S(1)} %collective-permute-done.3), channel_id=1, source_target_pairs={{0,4},{4,8},{8,12},{12,16},{16,20},{20,24},{24,28},{28,0},{1,5},{5... | collective-permute-start | bytes 92168 | tf_op jit(solution)/shard_map/ppermute | solution.py:26
  54.2 16.1 %collective-permute-start.5 = (bf16[48,320]{1,0:T(8,128)(2,1)S(1)}, bf16[48,320]{1,0:T(8,128)(2,1)S(1)}, u32[]{:S(2)}, u32[]{:S(2)}) collective-permute-start(bf16[48,320]{1,0:T(8,128)(2,1)S(1)} %collective-permute-done.4), channel_id=1, source_target_pairs={{0,4},{4,8},{8,12},{12,16},{16,20},{20,24},{24,28},{28,0},{1,5},{5... | collective-permute-start | bytes 92168 | tf_op jit(solution)/shard_map/ppermute | solution.py:26
  54.3 22.7 %copy-start.1 = (bf16[48,320]{1,0:T(8,128)(2,1)S(1)}, bf16[48,320]{1,0:T(8,128)(2,1)}, u32[]{:S(2)}) copy-start(bf16[48,320]{1,0:T(8,128)(2,1)} %param.6) | copy-start | bytes 92164
  54.3 22.8 %copy-start.2 = (f32[320]{0:T(512)S(1)}, f32[320]{0:T(512)}, u32[]{:S(2)}) copy-start(f32[320]{0:T(512)} %param.7) | copy-start | bytes 3844
  70.3 6.7 %collective-permute-start.6 = (bf16[48,320]{1,0:T(8,128)(2,1)S(1)}, bf16[48,320]{1,0:T(8,128)(2,1)S(1)}, u32[]{:S(2)}, u32[]{:S(2)}) collective-permute-start(bf16[48,320]{1,0:T(8,128)(2,1)S(1)} %collective-permute-done.5), channel_id=1, source_target_pairs={{0,4},{4,8},{8,12},{12,16},{16,20},{20,24},{24,28},{28,0},{1,5},{5... | collective-permute-start | bytes 92168 | tf_op jit(solution)/shard_map/ppermute | solution.py:26
Sparse Core Ops, SparseCore 0:
  40.1 33.3 all-reduce.3
  117.1 64.1 reduce-scatter.3
